TPU v7x, 32 devices: a whole 2x2x4 slice. The times are simulated.
32 devices in a mesh: gx: 4 (over y, core), gy: 8 (over z, x).
Axes of the slice: x: 2, y: 2, z: 4, core: 2. Of those that a mesh axis runs over, the one named last changes fastest.
Arguments:
- old_master: float32 [32, 128, 1536], P('gx', 'gy'), may hold values from -3 to 3
- old_first: float32 [32, 128, 1536], P('gx', 'gy'), may hold values from -3 to 3
- old_second: float32 [32, 128, 1536], P('gx', 'gy'), may hold values from 0.01 to 1
- new_grad: bfloat16 [32, 128, 1536], P(('gx', 'gy')), may hold values from -3072 to 3072
- counts: int32 [32, 32], P(None, ('gx', 'gy')), may hold values from 1 to 72, as said below
- old_owner: int32 [32], replicated, may hold values from 0 to 31, each once
- new_owner: int32 [32], replicated, may hold values from 0 to 31, each once
Outputs:
- new_master: float32 [32, 128, 1536], P(('gx', 'gy'))
- new_first: float32 [32, 128, 1536], P(('gx', 'gy'))
- new_second: float32 [32, 128, 1536], P(('gx', 'gy'))
Inputs may be any that keep to these rules, and one draw needn't show every extreme that they name: `old_owner`: every number of 0 to 31 appears once. `new_owner`: every number of 0 to 31 appears once. `counts`: every device routed at least one token to every expert.
All inputs are finite; a program needn't handle non-finite values.
Results may differ from a plain program's by a relative error of at most 0.0003.
Values sent between devices are 32-bit elements; how exact they have to be, the bound alone decides.
A program may use at most 64 MiB of HBM per device.

v0:
```python
import jax
import jax.numpy as jnp
from jax import lax
from jax.sharding import PartitionSpec as P

first_correction = 1.0 - 0.9**10
second_correction = 1.0 - 0.999**10


def adam_step(master, first, second, grad, slot_count):
    scaled = grad.astype(jnp.float32) / slot_count
    new_first = 0.9 * first + 0.1 * scaled
    new_second = 0.999 * second + 0.001 * scaled * scaled
    step_dir = new_first / first_correction / (jnp.sqrt(new_second / second_correction) + 1e-08)
    new_master = master - 0.01 * (step_dir + 0.1 * master)
    return (new_master, new_first, new_second)


def reorder(block, groups_x, groups_y):
    total_rows = block.shape[1]
    piece = total_rows // (groups_x * groups_y)
    shaped = block.reshape(1, groups_x, groups_y, piece, block.shape[2])
    return shaped.transpose(0, 2, 1, 3, 4).reshape(1, total_rows, block.shape[2])


def body(old_master, old_first, old_second, new_grad, counts, old_owner, new_owner):
    experts = old_owner.shape[0]
    groups_x = lax.axis_size("gx")
    groups_y = lax.axis_size("gy")
    my_slot = lax.axis_index("gx") * groups_y + lax.axis_index("gy")
    slots = jnp.arange(experts, dtype=jnp.int32)
    onehot = new_owner[:, None] == slots[None, :]
    source = jnp.sum(jnp.where(onehot, old_owner[:, None], 0), axis=0)
    local_counts = counts[:, 0].astype(jnp.float32)
    by_rows = (
        lax.all_to_all(old_master, "gx", split_axis=1, concat_axis=0, tiled=True),
        lax.all_to_all(old_first, "gx", split_axis=1, concat_axis=0, tiled=True),
        lax.all_to_all(old_second, "gx", split_axis=1, concat_axis=0, tiled=True),
    )
    permuted = tuple((jnp.take(state, source, axis=0) for state in by_rows))
    landed = lax.all_to_all(permuted, ("gx", "gy"), split_axis=0, concat_axis=1, tiled=True)
    arrived = tuple((reorder(state, groups_x, groups_y) for state in landed))
    totals = lax.psum(local_counts, ("gx", "gy"))
    slot_count = jnp.sum(jnp.where(new_owner == my_slot, totals, jnp.float32(0.0)))
    return adam_step(arrived[0], arrived[1], arrived[2], new_grad, slot_count)


def solution(mesh):
    placed = (
        P("gx", "gy", None),
        P("gx", "gy", None),
        P("gx", "gy", None),
        P(("gx", "gy"), None, None),
        P(None, ("gx", "gy")),
        P(),
        P(),
    )
    return jax.shard_map(
        body,
        mesh=mesh,
        in_specs=placed,
        out_specs=(
            P(("gx", "gy"), None, None),
            P(("gx", "gy"), None, None),
            P(("gx", "gy"), None, None),
        ),
        check_vma=False,
    )
```

profile of v0, /device:TPU:0, one launch (start us, length us, event | category | flops | bytes accessed | tf_op | source)
XLA Modules:
  0.0 156.1 jit_solution(17211418162359433335)
XLA Ops:
  0.6 2.5 %copy.67 = f32[8,16,1536]{2,0,1:T(8,128)} copy(f32[8,16,1536]{2,1,0:T(8,128)} %param.9) | data formatting | bytes 1572864 | tf_op args[0]
  3.1 0.0 copy-start
  3.1 4.4 %all-to-all-start = ((f32[8,16,1536]{2,0,1:T(8,128)}), f32[8,16,1536]{2,0,1:T(8,128)S(1)}, u32[]{:S(2)}, u32[]{:S(2)}) async-start(f32[8,16,1536]{2,0,1:T(8,128)} %copy.67), calls=%async_computation | async-start | bytes 1572864 | tf_op jit(solution)/shard_map/all_to_all | solution.py:36
  7.5 0.0 copy-done
  7.5 1.3 copy.72
  8.8 0.0 copy-start.1
  8.8 10.3 %all-to-all-done = f32[8,16,1536]{2,0,1:T(8,128)S(1)} async-done(((f32[8,16,1536]{2,0,1:T(8,128)}), f32[8,16,1536]{2,0,1:T(8,128)S(1)}, u32[]{:S(2)}, u32[]{:S(2)}) %all-to-all-start) | async-done | bytes 786464 | tf_op jit(solution)/shard_map/all_to_all | solution.py:36
  19.1 3.5 %all-to-all-start.2 = ((f32[8,16,1536]{2,0,1:T(8,128)}), f32[8,16,1536]{2,0,1:T(8,128)S(1)}, u32[]{:S(2)}, u32[]{:S(2)}) async-start(f32[8,16,1536]{2,0,1:T(8,128)} %copy.72), calls=%async_computation.2 | async-start | bytes 1572864 | tf_op jit(solution)/shard_map/all_to_all | solution.py:37
  22.6 0.0 copy-done.1
  22.6 1.3 copy.78
  24.0 0.0 copy-start.3
  24.0 0.0 copy-start.4
  24.0 10.2 %all-to-all-done.2 = f32[8,16,1536]{2,0,1:T(8,128)S(1)} async-done(((f32[8,16,1536]{2,0,1:T(8,128)}), f32[8,16,1536]{2,0,1:T(8,128)S(1)}, u32[]{:S(2)}, u32[]{:S(2)}) %all-to-all-start.2) | async-done | bytes 786464 | tf_op jit(solution)/shard_map/all_to_all | solution.py:37
  34.2 3.5 %all-to-all-start.4 = ((f32[8,16,1536]{2,0,1:T(8,128)}), f32[8,16,1536]{2,0,1:T(8,128)S(1)}, u32[]{:S(2)}, u32[]{:S(2)}) async-start(f32[8,16,1536]{2,0,1:T(8,128)} %copy.78), calls=%async_computation.4 | async-start | bytes 1572864 | tf_op jit(solution)/shard_map/all_to_all | solution.py:38
  37.7 0.0 copy-done.3
  37.7 0.0 copy-done.4
  37.7 0.1 select_reduce_fusion
  37.9 0.1 copy.104
  37.9 0.5 copy.69
  38.4 0.1 copy.102
  38.5 1.4 copy.74
  39.9 1.0 gather_fusion
  40.9 2.2 %gather_fusion.1 = f32[32,4,1536]{2,1,0:T(4,128)S(1)} fusion(f32[32,4,1536]{2,1,0:T(4,128)} %copy.74, s32[1024]{0:T(1024)S(1)} %pad_clamp_fusion), kind=kCustom, calls=%fused_computation.1.clone | custom fusion | bytes 1572992 | tf_op jit(solution)/shard_map/jit(_take)/gather | solution.py:40
  43.1 6.2 %all-to-all-done.4 = f32[8,16,1536]{2,0,1:T(8,128)S(1)} async-done(((f32[8,16,1536]{2,0,1:T(8,128)}), f32[8,16,1536]{2,0,1:T(8,128)S(1)}, u32[]{:S(2)}, u32[]{:S(2)}) %all-to-all-start.4) | async-done | bytes 786464 | tf_op jit(solution)/shard_map/all_to_all | solution.py:38
  49.3 0.1 copy.101
  49.4 0.5 copy.80
  49.9 1.0 gather_fusion.2
  50.9 1.5 broadcast_select_fusion
  52.4 27.2 %all_to_all.81 = f32[32,4,1536]{2,1,0:T(4,128)S(1)} all-to-all(f32[32,4,1536]{2,1,0:T(4,128)S(1)} %get-tuple-element.13), channel_id=1, replica_groups=mesh['gx'=4,'gy'=8] {'gx','gy'}, dimensions={0} | all-to-all | bytes 1572864 | tf_op jit(solution)/shard_map/all_to_all | solution.py:41
  79.6 24.0 %all_to_all.82 = f32[32,4,1536]{2,1,0:T(4,128)S(1)} all-to-all(f32[32,4,1536]{2,1,0:T(4,128)S(1)} %get-tuple-element.14), channel_id=1, replica_groups=mesh['gx'=4,'gy'=8] {'gx','gy'}, dimensions={0} | all-to-all | bytes 1572864 | tf_op jit(solution)/shard_map/all_to_all | solution.py:41
  103.6 0.0 copy-start.5
  103.6 2.8 %all-to-all-start.1 = ((f32[32,4,1536]{2,1,0:T(4,128)}), f32[32,4,1536]{2,1,0:T(4,128)S(1)}, u32[]{:S(2)}, u32[]{:S(2)}) async-start(f32[32,4,1536]{2,1,0:T(4,128)} %get-tuple-element.15), calls=%async_computation.1 | async-start | bytes 1572864 | tf_op jit(solution)/shard_map/all_to_all | solution.py:41
  106.4 0.0 copy-done.5
  106.4 43.1 %psum.7 = f32[32]{0:T(128)S(1)} all-reduce(f32[32]{0:T(128)S(1)} %convert_bitcast_fusion), channel_id=1, replica_groups=mesh['gx'=4,'gy'=8] {'gx','gy'}, use_global_device_ids=true, to_apply=%region_1.3 | all-reduce | flops 32 | bytes 256 | tf_op jit(solution)/shard_map/psum | solution.py:43
  149.5 0.7 fusion.3
  150.2 0.3 fusion.1
  150.5 0.8 copy.82
  151.3 0.3 fusion.2
  151.6 0.8 copy.76
  152.4 0.0 all-to-all-done.1
  152.4 0.3 copy.103
  152.7 0.0 copy-start.2
  152.7 0.8 copy.71
  153.5 0.2 copy-done.2
  153.7 2.5 %multiply_subtract_fusion = (f32[1,128,1536]{2,1,0:T(8,128)}, f32[1,128,1536]{2,1,0:T(8,128)}, f32[1,128,1536]{2,1,0:T(8,128)}) fusion(f32[1,128,1536]{2,0,1:T(1,128)S(1)} %bitcast.45, f32[]{:T(128)} %fusion.3, bf16[1,128,1536]{2,1,0:T(8,128)(2,1)S(1)} %copy-done.2, f32[1,128,1536]{2,0,1:T(1,128)S(1)} %bitcast.44, f32[1,128,1536]{2,0,1:T(1,128)S(1)} %bitcast.43), kind=kLoop, calls=%fused_computation.14 | loop fusion | flops 2949120 | bytes 5111812 | tf_op jit(solution)/shard_map/sub | solution.py:15
  (4 shorter events, 0.0 us)
Async XLA Ops:
  3.1 4.4 %copy-start = (f32[8,16,1536]{2,1,0:T(8,128)S(1)}, f32[8,16,1536]{2,1,0:T(8,128)}, u32[]{:S(2)}) copy-start(f32[8,16,1536]{2,1,0:T(8,128)} %param.10) | copy-start | bytes 2359300
  3.1 16.0 %all-to-all-start = ((f32[8,16,1536]{2,0,1:T(8,128)}), f32[8,16,1536]{2,0,1:T(8,128)S(1)}, u32[]{:S(2)}, u32[]{:S(2)}) async-start(f32[8,16,1536]{2,0,1:T(8,128)} %copy.67), calls=%async_computation | async-start | bytes 1572864 | tf_op jit(solution)/shard_map/all_to_all | solution.py:36
  8.8 13.8 %copy-start.1 = (f32[8,16,1536]{2,1,0:T(8,128)S(1)}, f32[8,16,1536]{2,1,0:T(8,128)}, u32[]{:S(2)}) copy-start(f32[8,16,1536]{2,1,0:T(8,128)} %param.11) | copy-start | bytes 2359300
  19.1 15.1 %all-to-all-start.2 = ((f32[8,16,1536]{2,0,1:T(8,128)}), f32[8,16,1536]{2,0,1:T(8,128)S(1)}, u32[]{:S(2)}, u32[]{:S(2)}) async-start(f32[8,16,1536]{2,0,1:T(8,128)} %copy.72), calls=%async_computation.2 | async-start | bytes 1572864 | tf_op jit(solution)/shard_map/all_to_all | solution.py:37
  24.0 13.7 %copy-start.3 = (s32[32]{0:T(128)S(1)}, s32[32]{0:T(128)}, u32[]{:S(2)}) copy-start(s32[32]{0:T(128)} %param.15) | copy-start | bytes 388
  24.0 13.8 %copy-start.4 = (s32[32]{0:T(128)S(1)}, s32[32]{0:T(128)}, u32[]{:S(2)}) copy-start(s32[32]{0:T(128)} %param.14) | copy-start | bytes 388
  34.2 15.1 %all-to-all-start.4 = ((f32[8,16,1536]{2,0,1:T(8,128)}), f32[8,16,1536]{2,0,1:T(8,128)S(1)}, u32[]{:S(2)}, u32[]{:S(2)}) async-start(f32[8,16,1536]{2,0,1:T(8,128)} %copy.78), calls=%async_computation.4 | async-start | bytes 1572864 | tf_op jit(solution)/shard_map/all_to_all | solution.py:38
  103.6 2.8 %copy-start.5 = (s32[32,1]{0,1:T(1,128)S(1)}, s32[32,1]{0,1:T(1,128)}, u32[]{:S(2)}) copy-start(s32[32,1]{0,1:T(1,128)} %param.13) | copy-start | bytes 388
  103.6 48.8 %all-to-all-start.1 = ((f32[32,4,1536]{2,1,0:T(4,128)}), f32[32,4,1536]{2,1,0:T(4,128)S(1)}, u32[]{:S(2)}, u32[]{:S(2)}) async-start(f32[32,4,1536]{2,1,0:T(4,128)} %get-tuple-element.15), calls=%async_computation.1 | async-start | bytes 1572864 | tf_op jit(solution)/shard_map/all_to_all | solution.py:41
  152.7 1.0 copy-start.2
where the time goes:
time: 157 us; the launch traced here: 156 us
  blocking collectives  94.3 us (60%)
  waiting for transfers between devices  26.7 us (17%)
  local copies, waits for them, and re-layouts  14.8 us (9%)
  starting transfers between devices  14.1 us (9%)
  other arithmetic  5.31 us (3%)
    all_to_all x2, blocking collectives, body(): lax.all_to_all(permuted, ('gx', 'gy'), split_axis=0, concat_axis=1, tiled...  51.2 us
    psum x1, blocking collectives, body(): totals = lax.psum(local_counts, ('gx', 'gy'))  43.1 us
    all_to_all x1, waiting for transfers between devices, body(): lax.all_to_all(old_master, 'gx', split_axis=1, concat_axis=0, tiled=True)  10.3 us
    all_to_all x1, waiting for transfers between devices, body(): lax.all_to_all(old_first, 'gx', split_axis=1, concat_axis=0, tiled=True)  10.2 us
    all_to_all x1, waiting for transfers between devices, body(): lax.all_to_all(old_second, 'gx', split_axis=1, concat_axis=0, tiled=True)  6.23 us
    unnamed x15, local copies, waits for them, and re-layouts  5.34 us
    all_to_all x1, starting transfers between devices, body(): lax.all_to_all(old_master, 'gx', split_axis=1, concat_axis=0, tiled=True)  4.4 us
    gather x3, local copies, waits for them, and re-layouts, body(): permuted = tuple((jnp.take(state, source, axis=0) for state in by_rows))  4.19 us
  transfers between devices with their start and end apart: 4, of which 3 were waited for; matrix products, arithmetic and copies ran while one was open for 7% of the time, Pallas kernels for 0%

commit v1 on v0

--- a/solution.py
+++ b/solution.py
@@ -5,6 +5,18 @@
 
 first_correction = 1.0 - 0.9**10
 second_correction = 1.0 - 0.999**10
+
+
+def rotated_exchange(array, axis, split, join):
+    ways, here = (lax.axis_size(axis), lax.axis_index(axis))
+    width = array.shape[split] // ways
+    turned = jnp.roll(array, -here * width, axis=split)
+    got = [lax.slice_in_dim(turned, 0, width, axis=split)]
+    for far in range(1, ways):
+        sent = lax.slice_in_dim(turned, far * width, (far + 1) * width, axis=split)
+        got.append(lax.ppermute(sent, axis, [(d, (d + far) % ways) for d in range(ways)]))
+    line = jnp.concatenate(got[::-1], axis=join)
+    return jnp.roll(line, (here + 1) * got[0].shape[join], axis=join)
 
 
 def adam_step(master, first, second, grad, slot_count):
@@ -35,7 +47,7 @@
     by_rows = (
         lax.all_to_all(old_master, "gx", split_axis=1, concat_axis=0, tiled=True),
         lax.all_to_all(old_first, "gx", split_axis=1, concat_axis=0, tiled=True),
-        lax.all_to_all(old_second, "gx", split_axis=1, concat_axis=0, tiled=True),
+        rotated_exchange(old_second, "gx", 1, 0),
     )
     permuted = tuple((jnp.take(state, source, axis=0) for state in by_rows))
     landed = lax.all_to_all(permuted, ("gx", "gy"), split_axis=0, concat_axis=1, tiled=True)

time: 157 us -> 145 us (0.924)
  waiting for transfers between devices: 26.7 us -> 13.8 us
    all_to_all x1 -> x0, waiting for transfers between devices: 6.23 us -> none  [body(): lax.all_to_all(old_second, 'gx', split_axis=1, concat_axis=0, tiled=True)]
    all_to_all x1, waiting for transfers between devices: 10.3 us -> 4.07 us  [body(): lax.all_to_all(old_master, 'gx', split_axis=1, concat_axis=0, tiled=True)]
    all_to_all x1 -> x0, starting transfers between devices: 3.49 us -> none  [body(): lax.all_to_all(old_second, 'gx', split_axis=1, concat_axis=0, tiled=True)]
    ppermute x0 -> x3, starting transfers between devices: none -> 3.43 us  [rotated_exchange(): lax.ppermute(sent, axis, [(d, (d + far) % ways) for d in range(ways)])]
    all_to_all x1, waiting for transfers between devices: 10.2 us -> 7.08 us  [body(): lax.all_to_all(old_first, 'gx', split_axis=1, concat_axis=0, tiled=True)]
    ppermute x0 -> x3, waiting for transfers between devices: none -> 2.7 us  [rotated_exchange(): lax.ppermute(sent, axis, [(d, (d + far) % ways) for d in range(ways)])]
    unnamed x15 -> x21, local copies, waits for them, and re-layouts: 5.34 us -> 7.56 us
  transfers between devices with their start and end apart: 4 -> 6, of which waited for: 3 -> 3; matrix products, arithmetic and copies ran while one was open for 7% -> 10% of each run, Pallas kernels for 0% -> 0%
where the time goes in v1:
time: 145 us; the launch traced here: 144 us
  blocking collectives  93.7 us (65%)
  local copies, waits for them, and re-layouts  15.9 us (11%)
  waiting for transfers between devices  13.8 us (10%)
  starting transfers between devices  13 us (9%)
  other arithmetic  6.63 us (5%)
    all_to_all x2, blocking collectives, body(): lax.all_to_all(permuted, ('gx', 'gy'), split_axis=0, concat_axis=1, tiled...  50.6 us
    psum x1, blocking collectives, body(): totals = lax.psum(local_counts, ('gx', 'gy'))  43.1 us
    unnamed x21, local copies, waits for them, and re-layouts  7.56 us
    all_to_all x1, waiting for transfers between devices, body(): lax.all_to_all(old_first, 'gx', split_axis=1, concat_axis=0, tiled=True)  7.08 us
    all_to_all x1, waiting for transfers between devices, body(): lax.all_to_all(old_master, 'gx', split_axis=1, concat_axis=0, tiled=True)  4.07 us
    all_to_all x1, starting transfers between devices, body(): lax.all_to_all(old_first, 'gx', split_axis=1, concat_axis=0, tiled=True)  3.49 us
    all_to_all x1, starting transfers between devices, body(): lax.all_to_all(old_master, 'gx', split_axis=1, concat_axis=0, tiled=True)  3.49 us
    ppermute x3, starting transfers between devices, rotated_exchange(): lax.ppermute(sent, axis, [(d, (d + far) % ways) for d in range(ways)])  3.43 us
  transfers between devices with their start and end apart: 6, of which 3 were waited for; matrix products, arithmetic and copies ran while one was open for 10% of the time, Pallas kernels for 0%

profile of v1, /device:TPU:0, one launch (start us, length us, event | category | flops | bytes accessed | tf_op | source)
XLA Modules:
  0.0 144.0 jit_solution(5343790603385558627)
XLA Ops:
  0.7 1.4 fusion.1
  2.1 0.1 fusion.5
  2.2 2.6 %collective-permute-start = (f32[8,4,1536]{2,1,0:T(4,128)S(1)}, f32[8,4,1536]{2,1,0:T(4,128)S(1)}, u32[]{:S(2)}, u32[]{:S(2)}) collective-permute-start(f32[8,4,1536]{2,1,0:T(4,128)S(1)} %get-tuple-element.15), channel_id=1, source_target_pairs={{0,24},{8,0},{16,8},{24,16},{1,25},{9,1},{17,9},{25,17},{2,26},{10... | collective-permute-start | bytes 589832 | tf_op jit(solution)/shard_map/ppermute | solution.py:17
  4.8 0.6 collective-permute-start.1
  5.5 0.2 collective-permute-start.2
  5.6 0.0 copy-done
  5.6 1.3 copy.56
  7.0 3.5 %all-to-all-start = ((f32[8,16,1536]{2,0,1:T(8,128)}), f32[8,16,1536]{2,0,1:T(8,128)S(1)}, u32[]{:S(2)}, u32[]{:S(2)}) async-start(f32[8,16,1536]{2,0,1:T(8,128)} %copy.56), calls=%async_computation | async-start | bytes 1572864 | tf_op jit(solution)/shard_map/all_to_all | solution.py:48
  10.5 0.1 select_reduce_fusion
  10.6 1.3 copy.61
  12.0 0.0 collective-permute-done
  12.0 0.7 constant_dynamic-update-slice_fusion.5
  12.7 2.7 %collective-permute-done.1 = f32[8,4,1536]{2,1,0:T(4,128)S(1)} collective-permute-done((f32[8,4,1536]{2,1,0:T(4,128)S(1)}, f32[8,4,1536]{2,1,0:T(4,128)S(1)}, u32[]{:S(2)}, u32[]{:S(2)}) %collective-permute-start.1) | collective-permute-done | bytes 196640 | tf_op jit(solution)/shard_map/ppermute | solution.py:17
  15.4 0.7 constant_dynamic-update-slice_fusion.4
  16.0 0.0 collective-permute-done.2
  16.1 0.7 constant_dynamic-update-slice_fusion.3
  16.7 0.7 slice_dynamic-update-slice_fusion
  17.4 0.7 constant_dynamic-update-slice_fusion.2
  18.1 0.7 constant_dynamic-update-slice_fusion.1
  18.8 0.7 constant_dynamic-update-slice_fusion
  19.5 4.1 %all-to-all-done = f32[8,16,1536]{2,0,1:T(8,128)S(1)} async-done(((f32[8,16,1536]{2,0,1:T(8,128)}), f32[8,16,1536]{2,0,1:T(8,128)S(1)}, u32[]{:S(2)}, u32[]{:S(2)}) %all-to-all-start) | async-done | bytes 786464 | tf_op jit(solution)/shard_map/all_to_all | solution.py:48
  23.6 3.5 %all-to-all-start.2 = ((f32[8,16,1536]{2,0,1:T(8,128)}), f32[8,16,1536]{2,0,1:T(8,128)S(1)}, u32[]{:S(2)}, u32[]{:S(2)}) async-start(f32[8,16,1536]{2,0,1:T(8,128)} %copy.61), calls=%async_computation.2 | async-start | bytes 1572864 | tf_op jit(solution)/shard_map/all_to_all | solution.py:49
  27.1 0.7 slice_dynamic-update-slice_fusion.1
  27.8 1.2 constant_dynamic-slice_fusion
  29.0 1.0 gather_fusion.2
  30.0 0.1 copy.83
  30.1 0.5 copy.58
  30.6 1.0 gather_fusion
  31.6 7.1 %all-to-all-done.2 = f32[8,16,1536]{2,0,1:T(8,128)S(1)} async-done(((f32[8,16,1536]{2,0,1:T(8,128)}), f32[8,16,1536]{2,0,1:T(8,128)S(1)}, u32[]{:S(2)}, u32[]{:S(2)}) %all-to-all-start.2) | async-done | bytes 786464 | tf_op jit(solution)/shard_map/all_to_all | solution.py:49
  38.7 0.1 copy.81
  38.8 0.5 copy.63
  39.3 1.0 gather_fusion.1
  40.3 1.5 %broadcast_select_fusion = (f32[32,4,1536]{2,1,0:T(4,128)S(1)}, f32[32,4,1536]{2,1,0:T(4,128)S(1)}, f32[32,4,1536]{2,1,0:T(4,128)}) fusion(f32[32,4,1536]{2,1,0:T(4,128)S(1)} %gather_fusion.2, pred[32]{0:T(512)(128)(4,1)S(1)} %compare_and_fusion, f32[32,4,1536]{2,1,0:T(4,128)S(1)} %gather_fusion.1, f32[32,4,1536]{2,1,0:T(4,128)S(1)} %gather_fusion), kind=kLoop, calls=%fused_computation.17 | loop fusion | flops 589824 | bytes 4718624 | tf_op jit(solution)/shard_map/jit(_take)/select_n | solution.py:52
  41.8 26.6 %all_to_all.63 = f32[32,4,1536]{2,1,0:T(4,128)S(1)} all-to-all(f32[32,4,1536]{2,1,0:T(4,128)S(1)} %get-tuple-element.16), channel_id=1, replica_groups=mesh['gx'=4,'gy'=8] {'gx','gy'}, dimensions={0} | all-to-all | bytes 1572864 | tf_op jit(solution)/shard_map/all_to_all | solution.py:53
  68.4 24.0 %all_to_all.64 = f32[32,4,1536]{2,1,0:T(4,128)S(1)} all-to-all(f32[32,4,1536]{2,1,0:T(4,128)S(1)} %get-tuple-element.17), channel_id=1, replica_groups=mesh['gx'=4,'gy'=8] {'gx','gy'}, dimensions={0} | all-to-all | bytes 1572864 | tf_op jit(solution)/shard_map/all_to_all | solution.py:53
  92.4 2.6 %all-to-all-start.1 = ((f32[32,4,1536]{2,1,0:T(4,128)}), f32[32,4,1536]{2,1,0:T(4,128)S(1)}, u32[]{:S(2)}, u32[]{:S(2)}) async-start(f32[32,4,1536]{2,1,0:T(4,128)} %get-tuple-element.18), calls=%async_computation.1 | async-start | bytes 1572864 | tf_op jit(solution)/shard_map/all_to_all | solution.py:53
  95.1 43.1 %psum.7 = f32[32]{0:T(128)S(1)} all-reduce(f32[32]{0:T(128)S(1)} %convert_bitcast_fusion), channel_id=1, replica_groups=mesh['gx'=4,'gy'=8] {'gx','gy'}, use_global_device_ids=true, to_apply=%region_1.3 | all-reduce | flops 32 | bytes 256 | tf_op jit(solution)/shard_map/psum | solution.py:55
  138.1 0.7 fusion.3
  138.8 0.2 broadcast_multiply_fusion
  139.0 0.1 copy.80
  139.1 0.3 mul.97
  139.4 0.3 fusion.2
  139.7 0.8 copy.65
  140.5 0.0 copy-start.2
  140.5 0.0 all-to-all-done.1
  140.5 0.3 copy.82
  140.8 0.8 copy.60
  141.6 2.4 %multiply_subtract_fusion = (f32[1,128,1536]{2,1,0:T(8,128)}, f32[1,128,1536]{2,1,0:T(8,128)}, f32[1,128,1536]{2,1,0:T(8,128)}) fusion(f32[1,128,1536]{2,0,1:T(1,128)S(1)} %bitcast.37, f32[]{:T(128)} %fusion.3, bf16[1,128,1536]{2,1,0:T(8,128)(2,1)S(1)} %copy-done.2, f32[1,128,1536]{2,0,1:T(1,128)S(1)} %bitcast.36, f32[1,128,1536]{2,1,0:T(8,128)S(1)} %mul.97), kind=kLoop, calls=%fused_computation.15 | loop fusion | flops 2949120 | bytes 5111812 | tf_op jit(solution)/shard_map/sub | solution.py:27
  (14 shorter events, 0.0 us)
Async XLA Ops:
  0.6 5.0 %copy-start = (f32[8,16,1536]{2,1,0:T(8,128)S(1)}, f32[8,16,1536]{2,1,0:T(8,128)}, u32[]{:S(2)}) copy-start(f32[8,16,1536]{2,1,0:T(8,128)} %param.9) | copy-start | bytes 2359300
  2.2 9.8 %collective-permute-start = (f32[8,4,1536]{2,1,0:T(4,128)S(1)}, f32[8,4,1536]{2,1,0:T(4,128)S(1)}, u32[]{:S(2)}, u32[]{:S(2)}) collective-permute-start(f32[8,4,1536]{2,1,0:T(4,128)S(1)} %get-tuple-element.15), channel_id=1, source_target_pairs={{0,24},{8,0},{16,8},{24,16},{1,25},{9,1},{17,9},{25,17},{2,26},{10... | collective-permute-start | bytes 589832 | tf_op jit(solution)/shard_map/ppermute | solution.py:17
  4.8 10.5 %collective-permute-start.1 = (f32[8,4,1536]{2,1,0:T(4,128)S(1)}, f32[8,4,1536]{2,1,0:T(4,128)S(1)}, u32[]{:S(2)}, u32[]{:S(2)}) collective-permute-start(f32[8,4,1536]{2,1,0:T(4,128)S(1)} %get-tuple-element.14), channel_id=1, source_target_pairs={{0,16},{8,24},{16,0},{24,8},{1,17},{9,25},{17,1},{25,9},{2,18},{10... | collective-permute-start | bytes 589832 | tf_op jit(solution)/shard_map/ppermute | solution.py:17
  5.5 5.0 %copy-start.3 = (s32[32]{0:T(128)S(1)}, s32[32]{0:T(128)}, u32[]{:S(2)}) copy-start(s32[32]{0:T(128)} %param.15) | copy-start | bytes 388
  5.5 5.0 %copy-start.4 = (s32[32]{0:T(128)S(1)}, s32[32]{0:T(128)}, u32[]{:S(2)}) copy-start(s32[32]{0:T(128)} %param.14) | copy-start | bytes 388
  5.5 5.1 %copy-start.1 = (f32[8,16,1536]{2,1,0:T(8,128)S(1)}, f32[8,16,1536]{2,1,0:T(8,128)}, u32[]{:S(2)}) copy-start(f32[8,16,1536]{2,1,0:T(8,128)} %param.10) | copy-start | bytes 2359300
  5.5 10.6 %collective-permute-start.2 = (f32[8,4,1536]{2,1,0:T(4,128)S(1)}, f32[8,4,1536]{2,1,0:T(4,128)S(1)}, u32[]{:S(2)}, u32[]{:S(2)}) collective-permute-start(f32[8,4,1536]{2,1,0:T(4,128)S(1)} %get-tuple-element.13), channel_id=1, source_target_pairs={{0,8},{8,16},{16,24},{24,0},{1,9},{9,17},{17,25},{25,1},{2,10},{10... | collective-permute-start | bytes 589832 | tf_op jit(solution)/shard_map/ppermute | solution.py:17
  7.0 16.6 %all-to-all-start = ((f32[8,16,1536]{2,0,1:T(8,128)}), f32[8,16,1536]{2,0,1:T(8,128)S(1)}, u32[]{:S(2)}, u32[]{:S(2)}) async-start(f32[8,16,1536]{2,0,1:T(8,128)} %copy.56), calls=%async_computation | async-start | bytes 1572864 | tf_op jit(solution)/shard_map/all_to_all | solution.py:48
  23.6 15.1 %all-to-all-start.2 = ((f32[8,16,1536]{2,0,1:T(8,128)}), f32[8,16,1536]{2,0,1:T(8,128)S(1)}, u32[]{:S(2)}, u32[]{:S(2)}) async-start(f32[8,16,1536]{2,0,1:T(8,128)} %copy.61), calls=%async_computation.2 | async-start | bytes 1572864 | tf_op jit(solution)/shard_map/all_to_all | solution.py:49
  68.4 26.6 %copy-start.5 = (s32[32,1]{0,1:T(1,128)S(1)}, s32[32,1]{0,1:T(1,128)}, u32[]{:S(2)}) copy-start(s32[32,1]{0,1:T(1,128)} %param.13) | copy-start | bytes 388
  92.4 48.1 %all-to-all-start.1 = ((f32[32,4,1536]{2,1,0:T(4,128)}), f32[32,4,1536]{2,1,0:T(4,128)S(1)}, u32[]{:S(2)}, u32[]{:S(2)}) async-start(f32[32,4,1536]{2,1,0:T(4,128)} %get-tuple-element.18), calls=%async_computation.1 | async-start | bytes 1572864 | tf_op jit(solution)/shard_map/all_to_all | solution.py:53
  140.5 1.1 copy-start.2
